TPU v7x, 32 devices: a whole 2x2x4 slice. The times are simulated.
32 devices in a mesh: seq: 8 (over y, x, core), dp: 4 (over z).
Axes of the slice: x: 2, y: 2, z: 4, core: 2. Of those that a mesh axis runs over, the one named last changes fastest.
Arguments:
- normed_input: bfloat16 [4, 1024, 2304], P('dp', 'seq'), may hold values from -6 to 6
- queries: bfloat16 [4, 1024, 2048], P('dp', 'seq'), may hold values from -9 to 9
- rotated_key_states: bfloat16 [4, 1024, 1024], P('dp', 'seq'), may hold values from -9 to 9
- value_head_states: bfloat16 [4, 1024, 1024], P('dp', 'seq'), may hold values from -6 to 6
- saved_attention_output: bfloat16 [4, 1024, 2048], P('dp', 'seq'), may hold values from -6 to 6
- output_cotangent: bfloat16 [4, 1024, 2048], P('dp', 'seq'), may hold values from -6 to 6
- doc_ids: int32 [4, 1024], P('dp', 'seq'), may hold values from 0 to 7, never falling along the last dimension, each value on 1 to 512 neighbouring positions
Outputs:
- query_grad: bfloat16 [4, 1024, 2048], P('dp', 'seq')
- key_grad: bfloat16 [4, 1024, 1024], P('dp', 'seq')
- value_weight_grad: float32 [2304, 1024], P(('seq', 'dp'))
Inputs may be any that keep to these rules, and one draw needn't show every extreme that they name: `doc_ids`: within each sequence document ids never fall; each document holds 1 to 512 positions.
All inputs are finite; a program needn't handle non-finite values.
Results may differ from a plain program's by a relative error of at most 0.009.
Values may be sent and summed in bfloat16 or wider, within the bound.
A program may use at most 128 MiB of HBM per device.

v0:
```python
import functools

import jax
import jax.numpy as jnp
from jax import lax
from jax.experimental import pallas as pl
from jax.experimental.pallas import tpu as pltpu
from jax.sharding import PartitionSpec as P

QUERY_HEADS = 16
KEY_VALUE_HEADS = 8
HEAD_WIDTH = 128
CORES = 2
MESH = pl.DeviceIdType.MESH

query_scale = 144.0 ** (-0.5)
soft_cap = 50.0


def flip(index, mask, count):
    out, bit = 0, 1
    while bit < count:
        digit = lax.rem(index // bit, 2)
        out = out + (1 - digit if mask & bit else digit) * bit
        bit *= 2
    return out


def at(index, width):
    start = index * width
    return pl.ds(start if isinstance(index, int) else pl.multiple_of(start, width), width)


def nt(a, b):
    return lax.dot_general(a, b, (((1,), (1,)), ((), ())), preferred_element_type=jnp.float32)


def tn(a, b):
    return lax.dot_general(a, b, (((0,), (0,)), ((), ())), preferred_element_type=jnp.float32)


def kernel(
    n, ndp, total_tokens,
    x_ref, q_ref, k_ref, v_ref, o_ref, do_ref, doc_ref,
    dq_out, dk_out, dw_out,
    rq, rk, rv, rdo, meta, rmeta, xt, rx, dock,
    dk_acc, dv_acc, dqs, dks, rdk, vg, pf, zs, zr,
    in_send, in_recv, local_sem, dq_send, dq_recv, dk_send, dk_recv, vg_send, vg_recv,
    fwd_send, fwd_recv, z_send, z_recv,
):
    me = lax.axis_index("seq")
    dme = lax.axis_index("dp")
    tokens = q_ref.shape[0]
    seq = n * tokens
    hw = HEAD_WIDTH
    group = QUERY_HEADS // KEY_VALUE_HEADS
    hq = QUERY_HEADS // n
    copies = group // hq
    rows = x_ref.shape[1] // n
    piece = rows // ndp
    chips = n // CORES
    width = CORES * hw // copies
    reach = (seq // 2 - 1 + tokens - 1) // tokens
    chip, core = me // CORES, lax.rem(me, CORES)
    partner = chip * CORES + (1 - core)

    barrier = pltpu.get_barrier_semaphore()
    for off in range(1, n):
        pl.semaphore_signal(barrier, inc=1, device_id={"seq": flip(me, off, n)}, device_id_type=MESH)
    for off in range(1, ndp):
        pl.semaphore_signal(
            barrier, inc=1, device_id={"dp": lax.rem(dme + off, ndp)}, device_id_type=MESH
        )
    pl.semaphore_wait(barrier, n - 1 + ndp - 1)

    def inputs(dest, slot):
        kv = dest * hq // group
        return [
            (k_ref.at[:, at(kv, hw)], rk.at[at(slot, tokens), :]),
            (v_ref.at[:, at(kv, hw)], rv.at[at(slot, tokens), :]),
            (q_ref.at[:, at(dest, hq * hw)], rq.at[at(slot, tokens), :]),
            (do_ref.at[:, at(dest, hq * hw)], rdo.at[at(slot, tokens), :]),
            (meta.at[dest], rmeta.at[slot]),
            (xt.at[at(dest, rows), :], rx.at[:, at(slot, tokens)]),
        ]

    def input_copy(kind, off):
        peer = flip(me, off, n)
        src, dst = inputs(peer, me)[kind]
        return pltpu.make_async_remote_copy(
            src_ref=src, dst_ref=dst, send_sem=in_send.at[kind, off], recv_sem=in_recv.at[kind, off],
            device_id={"seq": peer}, device_id_type=MESH,
        )

    def own_copy(kind):
        src, dst = inputs(me, me)[kind]
        return pltpu.make_async_copy(src, dst, local_sem.at[kind])

    def input_wait(kind, off):
        peer = flip(me, off, n)
        src, _ = inputs(peer, me)[kind]
        _, dst = inputs(peer, peer)[kind]
        pltpu.make_async_remote_copy(
            src_ref=src, dst_ref=dst, send_sem=in_send.at[kind, off], recv_sem=in_recv.at[kind, off],
            device_id={"seq": peer}, device_id_type=MESH,
        ).wait_recv()

    order = list(range(n - 1, 0, -1))
    for off in order:
        for kind in range(4):
            input_copy(kind, off).start()
    for kind in range(4):
        own_copy(kind).start()

    docs = doc_ref[...].astype(jnp.float32)
    for head in range(QUERY_HEADS):
        span = slice(head * hw, (head + 1) * hw)
        prod = do_ref[:, span].astype(jnp.float32) * o_ref[:, span].astype(jnp.float32)
        meta[head // hq, head % hq : head % hq + 1, :] = jnp.sum(prod.T, axis=0, keepdims=True)
    for dest in range(n):
        meta[dest, hq : hq + 1, :] = docs
        if hq + 1 < meta.shape[1]:
            meta[dest, hq + 1 :, :] = jnp.zeros((meta.shape[1] - hq - 1, tokens), jnp.float32)
    for off in order:
        input_copy(4, off).start()
    own_copy(4).start()
    for c in range(x_ref.shape[1] // hw):
        span = slice(c * hw, (c + 1) * hw)
        xt[span, :] = x_ref[:, span].astype(jnp.float32).T.astype(jnp.bfloat16)
    for off in order:
        input_copy(5, off).start()
    own_copy(5).start()

    for kind in range(5):
        own_copy(kind).wait()
    for off in order:
        for kind in range(5):
            input_wait(kind, off)

    def dk_slot(source):
        return rdk.at[lax.rem(source, copies), :, at(source // copies, hw)]

    def dq_copy(off, arriving=False):
        peer = flip(me, off, n)
        return pltpu.make_async_remote_copy(
            src_ref=dqs.at[peer], dst_ref=dq_out.at[:, at(peer if arriving else me, hq * hw)],
            send_sem=dq_send.at[off], recv_sem=dq_recv.at[off],
            device_id={"seq": peer}, device_id_type=MESH,
        )

    def dk_copy(off, arriving=False):
        peer = flip(me, off, n)
        return pltpu.make_async_remote_copy(
            src_ref=dks.at[peer], dst_ref=dk_slot(peer if arriving else me),
            send_sem=dk_send.at[off], recv_sem=dk_recv.at[off],
            device_id={"seq": peer}, device_id_type=MESH,
        )

    def dq_local():
        return pltpu.make_async_copy(dqs.at[me], dq_out.at[:, at(me, hq * hw)], local_sem.at[6])

    def dk_local():
        return pltpu.make_async_copy(dks.at[me], dk_slot(me), local_sem.at[7])

    def vg_slot(source, i):
        return vg.at[lax.rem(source, copies), at(i, tokens), at(source // copies, hw)]

    def vg_peer(c):
        return partner if c == 0 else flip(chip, c, chips) * CORES + core

    def vg_copy(c, i):
        return pltpu.make_async_remote_copy(
            src_ref=vg_slot(me, i), dst_ref=vg_slot(me, i),
            send_sem=vg_send.at[c, i], recv_sem=vg_recv.at[c, i],
            device_id={"seq": vg_peer(c)}, device_id_type=MESH,
        )

    def vg_wait(c, i):
        pltpu.make_async_remote_copy(
            src_ref=vg_slot(vg_peer(c), i), dst_ref=vg_slot(vg_peer(c), i),
            send_sem=vg_send.at[c, i], recv_sem=vg_recv.at[c, i],
            device_id={"seq": vg_peer(c)}, device_id_type=MESH,
        ).wait_recv()

    def fwd_slot(source):
        return vg.at[lax.rem(source, copies), :, at(source // copies, hw)]

    def fwd_copy(c, source):
        return pltpu.make_async_remote_copy(
            src_ref=fwd_slot(source), dst_ref=fwd_slot(source),
            send_sem=fwd_send.at[c], recv_sem=fwd_recv.at[c],
            device_id={"seq": partner}, device_id_type=MESH,
        )

    for j in range(n):
        dock[at(j, tokens), :] = jnp.broadcast_to(rmeta[j, hq : hq + 1, :], (tokens, tokens)).T

    causal = lax.broadcasted_iota(jnp.int32, (tokens, tokens), 0) <= lax.broadcasted_iota(
        jnp.int32, (tokens, tokens), 1
    )
    for i in reversed(range(n)):
        here = at(i, tokens)
        q2 = jnp.concatenate([rq[here, g * hw : (g + 1) * hw] for g in range(hq)], axis=0)
        do2 = jnp.concatenate([rdo[here, g * hw : (g + 1) * hw] for g in range(hq)], axis=0)
        delta = jnp.concatenate([rmeta[i, g : g + 1, :] for g in range(hq)], axis=1)
        docq = rmeta[i, hq : hq + 1, :]
        window = range(max(0, i - reach), i + 1)
        kept, totals = {}, jnp.zeros((1, hq * tokens), jnp.float32)
        for j in window:
            t = jnp.tanh(nt(rk[at(j, tokens), :], q2) * (query_scale / soft_cap))
            allowed = dock[at(j, tokens), :] == docq
            if i == j:
                allowed = allowed & causal
            mask = jnp.where(allowed, 1.0, 0.0)
            w = jnp.exp(soft_cap * t) * jnp.concatenate([mask] * hq, axis=1)
            totals = totals + jnp.sum(w, axis=0, keepdims=True)
            kept[j] = (t, w)
        inverse = 1.0 / totals
        dq = jnp.zeros((hq * tokens, hw), jnp.float32)
        for j in window:
            t, w = kept[j]
            kj = rk[at(j, tokens), :]
            p = w * inverse
            ds = p * (nt(rv[at(j, tokens), :], do2) - delta) * ((1.0 - t * t) * query_scale)
            ds16, p16 = ds.astype(jnp.bfloat16), p.astype(jnp.bfloat16)
            dk_term = jnp.dot(ds16, q2, preferred_element_type=jnp.float32)
            dv_term = jnp.dot(p16, do2, preferred_element_type=jnp.float32)
            if i == min(n - 1, j + reach):
                dk_acc[at(j, tokens), :] = dk_term
                dv_acc[at(j, tokens), :] = dv_term
            else:
                dk_acc[at(j, tokens), :] += dk_term
                dv_acc[at(j, tokens), :] += dv_term
            dq = dq + tn(ds16, kj)
        vg[lax.rem(me, copies), at(i, tokens), at(me // copies, hw)] = dv_acc[here, :].astype(jnp.bfloat16)
        for g in range(hq):
            dqs[i, :, g * hw : (g + 1) * hw] = dq[g * tokens : (g + 1) * tokens].astype(jnp.bfloat16)
        dks[i] = dk_acc[here, :].astype(jnp.bfloat16)
        for c in reversed(range(chips)):
            vg_copy(c, i).start()

    for off in order:
        dq_copy(off).start()
        dk_copy(off).start()
    dq_local().start()
    dk_local().start()

    own_copy(5).wait()
    for off in order:
        input_wait(5, off)

    def z_copy(c, off):
        dest = lax.rem(dme + off, ndp)
        return pltpu.make_async_remote_copy(
            src_ref=zs.at[c, dest], dst_ref=zr.at[c, dme],
            send_sem=z_send.at[c, off], recv_sem=z_recv.at[c, off],
            device_id={"dp": dest}, device_id_type=MESH,
        )

    def z_wait(c, off):
        source = lax.rem(dme + ndp - off, ndp)
        pltpu.make_async_remote_copy(
            src_ref=zs.at[c, source], dst_ref=zr.at[c, source],
            send_sem=z_send.at[c, off], recv_sem=z_recv.at[c, off],
            device_id={"dp": source}, device_id_type=MESH,
        ).wait_recv()

    for c in range(chips):
        if c == 0:
            for i in reversed(range(n)):
                vg_wait(0, i)
        else:
            for i in reversed(range(n)):
                vg_wait(c, i)
            fwd_copy(c, vg_peer(c)).start()
            fwd_copy(c, flip(chip, c, chips) * CORES + (1 - core)).wait_recv()
        columns = at(flip(chip, c, chips), width)
        values = vg[0, :, columns]
        if copies > 1:
            values = values.astype(jnp.float32)
            for other in range(1, copies):
                values = values + vg[other, :, columns].astype(jnp.float32)
            values = values.astype(jnp.bfloat16)
        pf[...] = jnp.dot(rx[...], values, preferred_element_type=jnp.float32)
        for d in range(ndp):
            zs[c, d] = pf[d * piece : (d + 1) * piece, :].astype(jnp.bfloat16)
        for off in range(1, ndp):
            z_copy(c, off).start()

    for off in order:
        dq_copy(off, True).wait()
        dk_copy(off, True).wait()
    dq_local().wait()
    dk_local().wait()

    total = rdk[0].astype(jnp.float32)
    for other in range(1, copies):
        total = total + rdk[other].astype(jnp.float32)
    dk_out[...] = total.astype(jnp.bfloat16)

    for c in range(chips):
        value = zs[c, dme].astype(jnp.float32)
        for off in range(1, ndp):
            z_wait(c, off)
            value = value + zr[c, lax.rem(dme + ndp - off, ndp)].astype(jnp.float32)
        dw_out[:, at(flip(chip, c, chips), width)] = value * total_tokens ** (-0.5)

    for off in order:
        for kind in range(6):
            input_copy(kind, off).wait_send()
    for c in range(chips):
        for i in range(n):
            vg_copy(c, i).wait_send()
        if c:
            fwd_copy(c, vg_peer(c)).wait_send()
        for off in range(1, ndp):
            z_copy(c, off).wait_send()


def solution(mesh):
    n, ndp = mesh.shape["seq"], mesh.shape["dp"]

    def local(normed_input, queries, keys, values, saved_output, cotangent, doc_ids):
        tokens = queries.shape[1]
        seq = n * tokens
        hw = HEAD_WIDTH
        hq = QUERY_HEADS // n
        copies = QUERY_HEADS // KEY_VALUE_HEADS // hq
        kvw = keys.shape[2]
        rows = normed_input.shape[2] // n
        piece = rows // ndp
        chips = n // CORES
        width = CORES * hw // copies
        bf, f32 = jnp.bfloat16, jnp.float32
        dma = pltpu.SemaphoreType.DMA
        vmem = pl.BlockSpec(memory_space=pltpu.VMEM)
        dq, dk, dw = pl.pallas_call(
            functools.partial(kernel, n, ndp, float(ndp * seq)),
            out_shape=(
                jax.ShapeDtypeStruct((tokens, queries.shape[2]), bf),
                jax.ShapeDtypeStruct((tokens, kvw), bf),
                jax.ShapeDtypeStruct((piece, kvw), f32),
            ),
            in_specs=[vmem] * 7,
            out_specs=(pl.BlockSpec(memory_space=pl.ANY), vmem, vmem),
            scratch_shapes=[
                pltpu.VMEM((seq, hq * hw), bf),
                pltpu.VMEM((seq, hw), bf),
                pltpu.VMEM((seq, hw), bf),
                pltpu.VMEM((seq, hq * hw), bf),
                pltpu.VMEM((n, 8, tokens), f32),
                pltpu.VMEM((n, 8, tokens), f32),
                pltpu.VMEM((n * rows, tokens), bf),
                pltpu.VMEM((rows, seq), bf),
                pltpu.VMEM((seq, tokens), f32),
                pltpu.VMEM((seq, hw), f32),
                pltpu.VMEM((seq, hw), f32),
                pltpu.VMEM((n, tokens, hq * hw), bf),
                pltpu.VMEM((n, tokens, hw), bf),
                pltpu.VMEM((copies, tokens, kvw), bf),
                pltpu.VMEM((copies, seq, kvw), bf),
                pltpu.VMEM((rows, width), f32),
                pltpu.VMEM((chips, ndp, piece, width), bf),
                pltpu.VMEM((chips, ndp, piece, width), bf),
                dma((6, n)), dma((6, n)), dma((8,)),
                dma((n,)), dma((n,)), dma((n,)), dma((n,)),
                dma((chips, n)), dma((chips, n)),
                dma((chips,)), dma((chips,)),
                dma((chips, ndp)), dma((chips, ndp)),
            ],
            compiler_params=pltpu.CompilerParams(
                collective_id=0, has_side_effects=True, vmem_limit_bytes=60 * 1024 * 1024
            ),
            name="attention_backward",
        )(normed_input[0], queries[0], keys[0], values[0], saved_output[0], cotangent[0], doc_ids)
        return dq[None], dk[None], dw

    spec = P("dp", "seq", None)
    return jax.shard_map(
        local,
        mesh=mesh,
        in_specs=(spec,) * 6 + (P("dp", "seq"),),
        out_specs=(spec, spec, P(("seq", "dp"), None)),
        check_vma=False,
    )
```

profile of v0, /device:TPU:1, one launch (start us, length us, event | category | flops | bytes accessed | tf_op | source)
XLA Modules:
  0.0 63.0 jit_solution(4788950555961057336)
XLA Ops:
  0.6 58.7 %attention_backward.1 = (bf16[128,2048]{1,0:T(8,128)(2,1)}, bf16[128,1024]{1,0:T(8,128)(2,1)}, f32[72,1024]{1,0:T(8,128)}) custom-call(bf16[128,2304]{1,0:T(8,128)(2,1)} %bitcast.8, bf16[128,2048]{1,0:T(8,128)(2,1)} %bitcast.10, bf16[128,1024]{1,0:T(8,128)(2,1)} %bitcast.13, bf16[128,1024]{1,0:T(8,128)(2,1)} %bitcast.14, bf16[128,2048]{1,0:T(8,128)(2,1)} %bitcast.11, ...), custom_call_target="tpu_custom_call" | custom-call | tf_op jit(solution)/shard_map/attention_backward/pallas_call | solution.py:337
  59.3 0.0 copy-start.1
  59.3 1.9 %copy.13 = bf16[1,128,2048]{2,1,0:T(8,128)(2,1)} copy(bf16[1,128,2048]{2,1,0:T(8,128)(2,1)} %bitcast.9) | data formatting | bytes 1048576
  61.2 0.0 copy-done.1
  61.2 0.0 copy-start
  61.2 0.7 %copy.14 = bf16[1,128,1024]{2,1,0:T(8,128)(2,1)} copy(bf16[1,128,1024]{2,1,0:T(8,128)(2,1)S(1)} %bitcast.15) | data formatting | bytes 524288
  61.9 0.4 copy-done
  62.3 0.7 %copy.15 = f32[72,1024]{1,0:T(8,128)} copy(f32[72,1024]{1,0:T(8,128)S(1)} %copy-done) | data formatting | bytes 589824
Async XLA Ops:
  59.3 1.9 %copy-start.1 = (bf16[128,1024]{1,0:T(8,128)(2,1)S(1)}, bf16[128,1024]{1,0:T(8,128)(2,1)}, u32[]{:S(2)}) copy-start(bf16[128,1024]{1,0:T(8,128)(2,1)} %get-tuple-element.7) | copy-start | bytes 786436
  61.2 1.1 %copy-start = (f32[72,1024]{1,0:T(8,128)S(1)}, f32[72,1024]{1,0:T(8,128)}, u32[]{:S(2)}) copy-start(f32[72,1024]{1,0:T(8,128)} %get-tuple-element.14) | copy-start | bytes 884740
where the time goes:
time: 63.3 us; the launch traced here: 63 us
  Pallas kernels  58.7 us (93%)
  local copies, waits for them, and re-layouts  3.7 us (6%)
  between operations  0.65 us (1%)
    pallas_call x1, Pallas kernels, local(): pl.pallas_call(functools.partial(kernel, n, ndp, float(ndp * seq)), out_s...  58.7 us
    unnamed x7, local copies, waits for them, and re-layouts  3.7 us

commit v1 on v0

--- a/solution.py
+++ b/solution.py
@@ -41,12 +41,13 @@
 
 def kernel(
     n, ndp, total_tokens,
+    x_in, q_in, k_in, v_in, o_in, do_in, doc_in,
+    dq_out, dk_out, dw_out,
     x_ref, q_ref, k_ref, v_ref, o_ref, do_ref, doc_ref,
-    dq_out, dk_out, dw_out,
     rq, rk, rv, rdo, meta, rmeta, xt, rx, dock,
     dk_acc, dv_acc, dqs, dks, rdk, vg, pf, zs, zr,
-    in_send, in_recv, local_sem, dq_send, dq_recv, dk_send, dk_recv, vg_send, vg_recv,
-    fwd_send, fwd_recv, z_send, z_recv,
+    load_sem, in_send, in_recv, local_sem, dq_send, dq_recv, dk_send, dk_recv, vg_send, vg_recv,
+    relay_send, relay_recv, fwd_send, fwd_recv, z_send, z_recv,
 ):
     me = lax.axis_index("seq")
     dme = lax.axis_index("dp")
@@ -65,21 +66,31 @@
     partner = chip * CORES + (1 - core)
 
     barrier = pltpu.get_barrier_semaphore()
-    for off in range(1, n):
-        pl.semaphore_signal(barrier, inc=1, device_id={"seq": flip(me, off, n)}, device_id_type=MESH)
     for off in range(1, ndp):
         pl.semaphore_signal(
             barrier, inc=1, device_id={"dp": lax.rem(dme + off, ndp)}, device_id_type=MESH
         )
-    pl.semaphore_wait(barrier, n - 1 + ndp - 1)
-
-    def inputs(dest, slot):
+    for off in range(n - 1, 0, -1):
+        pl.semaphore_signal(barrier, inc=1, device_id={"seq": flip(me, off, n)}, device_id_type=MESH)
+
+    loads = [
+        pltpu.make_async_copy(src, dst, load_sem.at[index])
+        for index, (src, dst) in enumerate((
+            (do_in, do_ref), (o_in, o_ref), (doc_in, doc_ref), (x_in, x_ref),
+            (k_in, k_ref), (v_in, v_ref), (q_in, q_ref),
+        ))
+    ]
+    for load in loads:
+        load.start()
+
+    def inputs(dest, slot, local=False):
         kv = dest * hq // group
+        sources = (k_in, v_in, q_in, do_in) if local else (k_ref, v_ref, q_ref, do_ref)
         return [
-            (k_ref.at[:, at(kv, hw)], rk.at[at(slot, tokens), :]),
-            (v_ref.at[:, at(kv, hw)], rv.at[at(slot, tokens), :]),
-            (q_ref.at[:, at(dest, hq * hw)], rq.at[at(slot, tokens), :]),
-            (do_ref.at[:, at(dest, hq * hw)], rdo.at[at(slot, tokens), :]),
+            (sources[0].at[:, at(kv, hw)], rk.at[at(slot, tokens), :]),
+            (sources[1].at[:, at(kv, hw)], rv.at[at(slot, tokens), :]),
+            (sources[2].at[:, at(dest, hq * hw)], rq.at[at(slot, tokens), :]),
+            (sources[3].at[:, at(dest, hq * hw)], rdo.at[at(slot, tokens), :]),
             (meta.at[dest], rmeta.at[slot]),
             (xt.at[at(dest, rows), :], rx.at[:, at(slot, tokens)]),
         ]
@@ -93,7 +104,7 @@
         )
 
     def own_copy(kind):
-        src, dst = inputs(me, me)[kind]
+        src, dst = inputs(me, me, True)[kind]
         return pltpu.make_async_copy(src, dst, local_sem.at[kind])
 
     def input_wait(kind, off):
@@ -105,13 +116,10 @@
             device_id={"seq": peer}, device_id_type=MESH,
         ).wait_recv()
 
-    order = list(range(n - 1, 0, -1))
-    for off in order:
-        for kind in range(4):
-            input_copy(kind, off).start()
     for kind in range(4):
         own_copy(kind).start()
-
+    for load in loads[:3]:
+        load.wait()
     docs = doc_ref[...].astype(jnp.float32)
     for head in range(QUERY_HEADS):
         span = slice(head * hw, (head + 1) * hw)
@@ -121,14 +129,21 @@
         meta[dest, hq : hq + 1, :] = docs
         if hq + 1 < meta.shape[1]:
             meta[dest, hq + 1 :, :] = jnp.zeros((meta.shape[1] - hq - 1, tokens), jnp.float32)
-    for off in order:
-        input_copy(4, off).start()
-    own_copy(4).start()
+    loads[3].wait()
     for c in range(x_ref.shape[1] // hw):
         span = slice(c * hw, (c + 1) * hw)
         xt[span, :] = x_ref[:, span].astype(jnp.float32).T.astype(jnp.bfloat16)
+    for load in loads[4:]:
+        load.wait()
+    pl.semaphore_wait(barrier, n - 1 + ndp - 1)
+
+    order = list(range(n - 1, 0, -1))
+    for off in order:
+        for kind in range(5):
+            input_copy(kind, off).start()
     for off in order:
         input_copy(5, off).start()
+    own_copy(4).start()
     own_copy(5).start()
 
     for kind in range(5):
@@ -138,6 +153,8 @@
             input_wait(kind, off)
 
     def dk_slot(source):
+        if copies == 1:
+            return dk_out.at[:, at(source, hw)]
         return rdk.at[lax.rem(source, copies), :, at(source // copies, hw)]
 
     def dq_copy(off, arriving=False):
@@ -165,21 +182,45 @@
     def vg_slot(source, i):
         return vg.at[lax.rem(source, copies), at(i, tokens), at(source // copies, hw)]
 
-    def vg_peer(c):
+    def chip_peer(c):
         return partner if c == 0 else flip(chip, c, chips) * CORES + core
 
     def vg_copy(c, i):
         return pltpu.make_async_remote_copy(
             src_ref=vg_slot(me, i), dst_ref=vg_slot(me, i),
             send_sem=vg_send.at[c, i], recv_sem=vg_recv.at[c, i],
-            device_id={"seq": vg_peer(c)}, device_id_type=MESH,
+            device_id={"seq": chip_peer(c)}, device_id_type=MESH,
         )
 
     def vg_wait(c, i):
         pltpu.make_async_remote_copy(
-            src_ref=vg_slot(vg_peer(c), i), dst_ref=vg_slot(vg_peer(c), i),
+            src_ref=vg_slot(chip_peer(c), i), dst_ref=vg_slot(chip_peer(c), i),
             send_sem=vg_send.at[c, i], recv_sem=vg_recv.at[c, i],
-            device_id={"seq": vg_peer(c)}, device_id_type=MESH,
+            device_id={"seq": chip_peer(c)}, device_id_type=MESH,
+        ).wait_recv()
+
+    direct = [c for c in range(chips) if c < 2 or c % 2 == 0]
+    evens = [c for c in direct if c > 1]
+
+    def relay_copy(c, half, i):
+        source, target = (1, c - 1) if half == 0 else (c - 1, 1)
+        start = i * tokens + half * (tokens // 2)
+        origin = chip_peer(source)
+        slot = vg.at[lax.rem(origin, copies), at(start // (tokens // 2), tokens // 2), at(origin // copies, hw)]
+        return pltpu.make_async_remote_copy(
+            src_ref=slot, dst_ref=slot,
+            send_sem=relay_send.at[c, half, i], recv_sem=relay_recv.at[c, half, i],
+            device_id={"seq": chip_peer(target)}, device_id_type=MESH,
+        )
+
+    def relay_wait(c, half, i):
+        origin = chip_peer(c)
+        start = i * tokens + half * (tokens // 2)
+        slot = vg.at[lax.rem(origin, copies), at(start // (tokens // 2), tokens // 2), at(origin // copies, hw)]
+        pltpu.make_async_remote_copy(
+            src_ref=slot, dst_ref=slot,
+            send_sem=relay_send.at[c, half, i], recv_sem=relay_recv.at[c, half, i],
+            device_id={"seq": chip_peer(1)}, device_id_type=MESH,
         ).wait_recv()
 
     def fwd_slot(source):
@@ -236,12 +277,15 @@
         for g in range(hq):
             dqs[i, :, g * hw : (g + 1) * hw] = dq[g * tokens : (g + 1) * tokens].astype(jnp.bfloat16)
         dks[i] = dk_acc[here, :].astype(jnp.bfloat16)
-        for c in reversed(range(chips)):
+        for c in reversed(direct):
             vg_copy(c, i).start()
 
-    for off in order:
+    def out_start(off):
         dq_copy(off).start()
         dk_copy(off).start()
+
+    outgoing = list(range(3, n, 2)) + list(range(2, n, 2)) + [1]
+    early = outgoing[:2]
     dq_local().start()
     dk_local().start()
 
@@ -265,15 +309,7 @@
             device_id={"dp": source}, device_id_type=MESH,
         ).wait_recv()
 
-    for c in range(chips):
-        if c == 0:
-            for i in reversed(range(n)):
-                vg_wait(0, i)
-        else:
-            for i in reversed(range(n)):
-                vg_wait(c, i)
-            fwd_copy(c, vg_peer(c)).start()
-            fwd_copy(c, flip(chip, c, chips) * CORES + (1 - core)).wait_recv()
+    def weight_term(c):
         columns = at(flip(chip, c, chips), width)
         values = vg[0, :, columns]
         if copies > 1:
@@ -287,18 +323,42 @@
         for off in range(1, ndp):
             z_copy(c, off).start()
 
-    for off in order:
-        dq_copy(off, True).wait()
-        dk_copy(off, True).wait()
-    dq_local().wait()
-    dk_local().wait()
-
-    total = rdk[0].astype(jnp.float32)
-    for other in range(1, copies):
-        total = total + rdk[other].astype(jnp.float32)
-    dk_out[...] = total.astype(jnp.bfloat16)
-
+    for i in reversed(range(n)):
+        vg_wait(0, i)
+    weight_term(0)
+    for i in reversed(range(n)):
+        if chips > 1:
+            vg_wait(1, i)
+        for c in evens:
+            if c + 1 < chips:
+                relay_copy(c + 1, 0, i).start()
+        for c in evens:
+            vg_wait(c, i)
+            if c + 1 < chips:
+                relay_copy(c + 1, 1, i).start()
+        if i == n // 2:
+            for off in early:
+                out_start(off)
+    for off in outgoing:
+        if off not in early:
+            out_start(off)
+    for c in direct:
+        if c:
+            fwd_copy(c, chip_peer(c)).start()
+    for c in direct:
+        if c:
+            fwd_copy(c, flip(chip, c, chips) * CORES + (1 - core)).wait_recv()
+            weight_term(c)
     for c in range(chips):
+        if c not in direct:
+            for i in reversed(range(n)):
+                relay_wait(c, 0, i)
+                relay_wait(c, 1, i)
+            fwd_copy(c, chip_peer(c)).start()
+            fwd_copy(c, flip(chip, c, chips) * CORES + (1 - core)).wait_recv()
+            weight_term(c)
+
+    for c in direct + [c for c in range(chips) if c not in direct]:
         value = zs[c, dme].astype(jnp.float32)
         for off in range(1, ndp):
             z_wait(c, off)
@@ -306,13 +366,29 @@
         dw_out[:, at(flip(chip, c, chips), width)] = value * total_tokens ** (-0.5)
 
     for off in order:
+        dq_copy(off, True).wait()
+        dk_copy(off, True).wait()
+    dq_local().wait()
+    dk_local().wait()
+
+    if copies > 1:
+        total = rdk[0].astype(jnp.float32)
+        for other in range(1, copies):
+            total = total + rdk[other].astype(jnp.float32)
+        dk_out[...] = total.astype(jnp.bfloat16)
+
+    for off in order:
         for kind in range(6):
             input_copy(kind, off).wait_send()
     for c in range(chips):
         for i in range(n):
-            vg_copy(c, i).wait_send()
+            if c in direct:
+                vg_copy(c, i).wait_send()
+            else:
+                relay_copy(c, 0, i).wait_send()
+                relay_copy(c, 1, i).wait_send()
         if c:
-            fwd_copy(c, vg_peer(c)).wait_send()
+            fwd_copy(c, chip_peer(c)).wait_send()
         for off in range(1, ndp):
             z_copy(c, off).wait_send()
 
@@ -337,13 +413,20 @@
         dq, dk, dw = pl.pallas_call(
             functools.partial(kernel, n, ndp, float(ndp * seq)),
             out_shape=(
-                jax.ShapeDtypeStruct((tokens, queries.shape[2]), bf),
-                jax.ShapeDtypeStruct((tokens, kvw), bf),
-                jax.ShapeDtypeStruct((piece, kvw), f32),
+                pltpu.VMEM((tokens, queries.shape[2]), bf),
+                pltpu.VMEM((tokens, kvw), bf),
+                pltpu.VMEM((piece, kvw), f32),
             ),
-            in_specs=[vmem] * 7,
-            out_specs=(pl.BlockSpec(memory_space=pl.ANY), vmem, vmem),
+            in_specs=[pl.BlockSpec(memory_space=pl.ANY)] * 7,
+            out_specs=(vmem, vmem, vmem),
             scratch_shapes=[
+                pltpu.VMEM((tokens, normed_input.shape[2]), bf),
+                pltpu.VMEM((tokens, queries.shape[2]), bf),
+                pltpu.VMEM((tokens, kvw), bf),
+                pltpu.VMEM((tokens, kvw), bf),
+                pltpu.VMEM((tokens, queries.shape[2]), bf),
+                pltpu.VMEM((tokens, queries.shape[2]), bf),
+                pltpu.VMEM((1, tokens), jnp.int32),
                 pltpu.VMEM((seq, hq * hw), bf),
                 pltpu.VMEM((seq, hw), bf),
                 pltpu.VMEM((seq, hw), bf),
@@ -362,10 +445,10 @@
                 pltpu.VMEM((rows, width), f32),
                 pltpu.VMEM((chips, ndp, piece, width), bf),
                 pltpu.VMEM((chips, ndp, piece, width), bf),
-                dma((6, n)), dma((6, n)), dma((8,)),
+                dma((7,)), dma((6, n)), dma((6, n)), dma((8,)),
                 dma((n,)), dma((n,)), dma((n,)), dma((n,)),
                 dma((chips, n)), dma((chips, n)),
-                dma((chips,)), dma((chips,)),
+                dma((chips, 2, n)), dma((chips, 2, n)), dma((chips,)), dma((chips,)),
                 dma((chips, ndp)), dma((chips, ndp)),
             ],
             compiler_params=pltpu.CompilerParams(

time: 63.3 us -> 55.4 us (0.88)
  Pallas kernels: 58.7 us -> 52.2 us
  local copies, waits for them, and re-layouts: 3.7 us -> 2.21 us
    pallas_call x1, Pallas kernels: 58.7 us -> 52.2 us  [local(): pl.pallas_call(functools.partial(kernel, n, ndp, float(ndp * seq)), out_s...]
    unnamed x7 -> x3, local copies, waits for them, and re-layouts: 3.7 us -> 2.21 us
where the time goes in v1:
time: 55.4 us; the launch traced here: 55 us
  Pallas kernels  52.2 us (94%)
  local copies, waits for them, and re-layouts  2.21 us (4%)
  between operations  0.64 us (1%)
    pallas_call x1, Pallas kernels, local(): pl.pallas_call(functools.partial(kernel, n, ndp, float(ndp * seq)), out_s...  52.2 us
    unnamed x3, local copies, waits for them, and re-layouts  2.21 us

profile of v1, /device:TPU:1, one launch (start us, length us, event | category | flops | bytes accessed | tf_op | source)
XLA Modules:
  0.0 55.0 jit_solution(4023889655100052774)
XLA Ops:
  0.6 52.2 %attention_backward.1 = (bf16[128,2048]{1,0:T(8,128)(2,1)S(1)}, bf16[128,1024]{1,0:T(8,128)(2,1)S(1)}, f32[72,1024]{1,0:T(8,128)S(1)}) custom-call(bf16[128,2304]{1,0:T(8,128)(2,1)} %bitcast.10, bf16[128,2048]{1,0:T(8,128)(2,1)} %bitcast.11, bf16[128,1024]{1,0:T(8,128)(2,1)} %bitcast.14, bf16[128,1024]{1,0:T(8,128)(2,1)} %bitcast.15, ...), custom_call_target="tpu_custom_call" | custom-call | tf_op jit(solution)/shard_map/attention_backward/pallas_call | solution.py:413
  52.8 0.8 %copy.13 = bf16[1,128,2048]{2,1,0:T(8,128)(2,1)} copy(bf16[1,128,2048]{2,1,0:T(8,128)(2,1)S(1)} %bitcast.8) | data formatting | bytes 1048576
  53.6 0.7 %copy.14 = bf16[1,128,1024]{2,1,0:T(8,128)(2,1)} copy(bf16[1,128,1024]{2,1,0:T(8,128)(2,1)S(1)} %bitcast.9) | data formatting | bytes 524288
  54.3 0.7 %copy.15 = f32[72,1024]{1,0:T(8,128)} copy(f32[72,1024]{1,0:T(8,128)S(1)} %get-tuple-element.11) | data formatting | bytes 589824

commit v2 on v1

--- a/solution.py
+++ b/solution.py
@@ -11,6 +11,7 @@
 KEY_VALUE_HEADS = 8
 HEAD_WIDTH = 128
 CORES = 2
+EARLY, MIDDLE = 2, 2
 MESH = pl.DeviceIdType.MESH
 
 query_scale = 144.0 ** (-0.5)
@@ -46,8 +47,8 @@
     x_ref, q_ref, k_ref, v_ref, o_ref, do_ref, doc_ref,
     rq, rk, rv, rdo, meta, rmeta, xt, rx, dock,
     dk_acc, dv_acc, dqs, dks, rdk, vg, pf, zs, zr,
-    load_sem, in_send, in_recv, local_sem, dq_send, dq_recv, dk_send, dk_recv, vg_send, vg_recv,
-    relay_send, relay_recv, fwd_send, fwd_recv, z_send, z_recv,
+    load_sem, in_send, in_recv, local_sem, out_send, out_recv, vg_send, near_recv, vg_recv,
+    relay_recv, fwd_recv, z_recv, seq_sem, dp_sem,
 ):
     me = lax.axis_index("seq")
     dme = lax.axis_index("dp")
@@ -65,13 +66,22 @@
     chip, core = me // CORES, lax.rem(me, CORES)
     partner = chip * CORES + (1 - core)
 
+    bits = [1 << b for b in range(n.bit_length() - 1)]
+    below, above = dme > 0, dme < ndp - 1
     barrier = pltpu.get_barrier_semaphore()
-    for off in range(1, ndp):
-        pl.semaphore_signal(
-            barrier, inc=1, device_id={"dp": lax.rem(dme + off, ndp)}, device_id_type=MESH
-        )
-    for off in range(n - 1, 0, -1):
-        pl.semaphore_signal(barrier, inc=1, device_id={"seq": flip(me, off, n)}, device_id_type=MESH)
+    for bit in reversed(bits):
+        pl.semaphore_signal(barrier, inc=1, device_id={"seq": flip(me, bit, n)}, device_id_type=MESH)
+
+    def tell_dp(up, down):
+        @pl.when(above)
+        def _():
+            pl.semaphore_signal(up, inc=1, device_id={"dp": dme + 1}, device_id_type=MESH)
+
+        @pl.when(below)
+        def _():
+            pl.semaphore_signal(down, inc=1, device_id={"dp": dme - 1}, device_id_type=MESH)
+
+    tell_dp(barrier, barrier)
 
     loads = [
         pltpu.make_async_copy(src, dst, load_sem.at[index])
@@ -99,7 +109,7 @@
         peer = flip(me, off, n)
         src, dst = inputs(peer, me)[kind]
         return pltpu.make_async_remote_copy(
-            src_ref=src, dst_ref=dst, send_sem=in_send.at[kind, off], recv_sem=in_recv.at[kind, off],
+            src_ref=src, dst_ref=dst, send_sem=in_send.at[kind], recv_sem=in_recv.at[kind],
             device_id={"seq": peer}, device_id_type=MESH,
         )
 
@@ -107,14 +117,17 @@
         src, dst = inputs(me, me, True)[kind]
         return pltpu.make_async_copy(src, dst, local_sem.at[kind])
 
-    def input_wait(kind, off):
-        peer = flip(me, off, n)
-        src, _ = inputs(peer, me)[kind]
-        _, dst = inputs(peer, peer)[kind]
-        pltpu.make_async_remote_copy(
-            src_ref=src, dst_ref=dst, send_sem=in_send.at[kind, off], recv_sem=in_recv.at[kind, off],
-            device_id={"seq": peer}, device_id_type=MESH,
-        ).wait_recv()
+    def bulk(ref, sem):
+        return pltpu.make_async_remote_copy(
+            src_ref=ref, dst_ref=ref, send_sem=sem, recv_sem=sem,
+            device_id={"seq": partner}, device_id_type=MESH,
+        )
+
+    rest = pl.ds(0, (n - 1) * tokens)
+    others = [
+        rk.at[rest, :], rv.at[rest, :], rq.at[rest, :], rdo.at[rest, :], rmeta.at[pl.ds(0, n - 1)],
+        xt.at[pl.ds(0, (n - 1) * rows), :],
+    ]
 
     for kind in range(4):
         own_copy(kind).start()
@@ -135,41 +148,59 @@
         xt[span, :] = x_ref[:, span].astype(jnp.float32).T.astype(jnp.bfloat16)
     for load in loads[4:]:
         load.wait()
-    pl.semaphore_wait(barrier, n - 1 + ndp - 1)
-
-    order = list(range(n - 1, 0, -1))
-    for off in order:
-        for kind in range(5):
-            input_copy(kind, off).start()
-    for off in order:
+    pl.semaphore_wait(barrier, len(bits) + below.astype(jnp.int32) + above.astype(jnp.int32))
+
+    for distance in range(1, len(bits) + 1):
+        if distance > 1:
+            for b, bit in enumerate(bits):
+                pl.semaphore_signal(
+                    seq_sem.at[distance - 2, b], inc=1, device_id={"seq": flip(me, bit, n)}, device_id_type=MESH
+                )
+            for b in range(len(bits)):
+                pl.semaphore_wait(seq_sem.at[distance - 2, b], 1)
+        for off in range(n - 1, 0, -1):
+            if off.bit_count() == distance:
+                for kind in range(5):
+                    input_copy(kind, off).start()
+    for off in range(n - 1, 0, -1):
         input_copy(5, off).start()
     own_copy(4).start()
     own_copy(5).start()
 
+    for step in range(ndp - 2):
+        tell_dp(dp_sem.at[step, 0], dp_sem.at[step, 1])
+
+        @pl.when(below)
+        def _():
+            pl.semaphore_wait(dp_sem.at[step, 0], 1)
+
+        @pl.when(above)
+        def _():
+            pl.semaphore_wait(dp_sem.at[step, 1], 1)
+
     for kind in range(5):
         own_copy(kind).wait()
-    for off in order:
-        for kind in range(5):
-            input_wait(kind, off)
+    for kind in range(5):
+        bulk(others[kind], in_recv.at[kind]).wait_recv()
 
     def dk_slot(source):
         if copies == 1:
             return dk_out.at[:, at(source, hw)]
         return rdk.at[lax.rem(source, copies), :, at(source // copies, hw)]
 
-    def dq_copy(off, arriving=False):
+    def dq_copy(off):
         peer = flip(me, off, n)
         return pltpu.make_async_remote_copy(
-            src_ref=dqs.at[peer], dst_ref=dq_out.at[:, at(peer if arriving else me, hq * hw)],
-            send_sem=dq_send.at[off], recv_sem=dq_recv.at[off],
+            src_ref=dqs.at[peer], dst_ref=dq_out.at[:, at(me, hq * hw)],
+            send_sem=out_send.at[0], recv_sem=out_recv.at[0],
             device_id={"seq": peer}, device_id_type=MESH,
         )
 
-    def dk_copy(off, arriving=False):
+    def dk_copy(off):
         peer = flip(me, off, n)
         return pltpu.make_async_remote_copy(
-            src_ref=dks.at[peer], dst_ref=dk_slot(peer if arriving else me),
-            send_sem=dk_send.at[off], recv_sem=dk_recv.at[off],
+            src_ref=dks.at[peer], dst_ref=dk_slot(me),
+            send_sem=out_send.at[1], recv_sem=out_recv.at[1],
             device_id={"seq": peer}, device_id_type=MESH,
         )
 
@@ -185,19 +216,15 @@
     def chip_peer(c):
         return partner if c == 0 else flip(chip, c, chips) * CORES + core
 
+    def vg_arrival(c, i):
+        return near_recv.at[0] if c == 0 else vg_recv.at[c // 2, i]
+
     def vg_copy(c, i):
         return pltpu.make_async_remote_copy(
             src_ref=vg_slot(me, i), dst_ref=vg_slot(me, i),
-            send_sem=vg_send.at[c, i], recv_sem=vg_recv.at[c, i],
+            send_sem=vg_send.at[0], recv_sem=vg_arrival(c, i),
             device_id={"seq": chip_peer(c)}, device_id_type=MESH,
         )
-
-    def vg_wait(c, i):
-        pltpu.make_async_remote_copy(
-            src_ref=vg_slot(chip_peer(c), i), dst_ref=vg_slot(chip_peer(c), i),
-            send_sem=vg_send.at[c, i], recv_sem=vg_recv.at[c, i],
-            device_id={"seq": chip_peer(c)}, device_id_type=MESH,
-        ).wait_recv()
 
     direct = [c for c in range(chips) if c < 2 or c % 2 == 0]
     evens = [c for c in direct if c > 1]
@@ -209,19 +236,9 @@
         slot = vg.at[lax.rem(origin, copies), at(start // (tokens // 2), tokens // 2), at(origin // copies, hw)]
         return pltpu.make_async_remote_copy(
             src_ref=slot, dst_ref=slot,
-            send_sem=relay_send.at[c, half, i], recv_sem=relay_recv.at[c, half, i],
+            send_sem=vg_send.at[1], recv_sem=relay_recv.at[c // 2],
             device_id={"seq": chip_peer(target)}, device_id_type=MESH,
         )
-
-    def relay_wait(c, half, i):
-        origin = chip_peer(c)
-        start = i * tokens + half * (tokens // 2)
-        slot = vg.at[lax.rem(origin, copies), at(start // (tokens // 2), tokens // 2), at(origin // copies, hw)]
-        pltpu.make_async_remote_copy(
-            src_ref=slot, dst_ref=slot,
-            send_sem=relay_send.at[c, half, i], recv_sem=relay_recv.at[c, half, i],
-            device_id={"seq": chip_peer(1)}, device_id_type=MESH,
-        ).wait_recv()
 
     def fwd_slot(source):
         return vg.at[lax.rem(source, copies), :, at(source // copies, hw)]
@@ -229,7 +246,7 @@
     def fwd_copy(c, source):
         return pltpu.make_async_remote_copy(
             src_ref=fwd_slot(source), dst_ref=fwd_slot(source),
-            send_sem=fwd_send.at[c], recv_sem=fwd_recv.at[c],
+            send_sem=vg_send.at[2], recv_sem=fwd_recv.at[c],
             device_id={"seq": partner}, device_id_type=MESH,
         )
 
@@ -285,29 +302,19 @@
         dk_copy(off).start()
 
     outgoing = list(range(3, n, 2)) + list(range(2, n, 2)) + [1]
-    early = outgoing[:2]
     dq_local().start()
     dk_local().start()
 
     own_copy(5).wait()
-    for off in order:
-        input_wait(5, off)
+    bulk(others[5], in_recv.at[5]).wait_recv()
 
     def z_copy(c, off):
         dest = lax.rem(dme + off, ndp)
         return pltpu.make_async_remote_copy(
             src_ref=zs.at[c, dest], dst_ref=zr.at[c, dme],
-            send_sem=z_send.at[c, off], recv_sem=z_recv.at[c, off],
+            send_sem=vg_send.at[3], recv_sem=z_recv.at[c],
             device_id={"dp": dest}, device_id_type=MESH,
         )
-
-    def z_wait(c, off):
-        source = lax.rem(dme + ndp - off, ndp)
-        pltpu.make_async_remote_copy(
-            src_ref=zs.at[c, source], dst_ref=zr.at[c, source],
-            send_sem=z_send.at[c, off], recv_sem=z_recv.at[c, off],
-            device_id={"dp": source}, device_id_type=MESH,
-        ).wait_recv()
 
     def weight_term(c):
         columns = at(flip(chip, c, chips), width)
@@ -323,51 +330,49 @@
         for off in range(1, ndp):
             z_copy(c, off).start()
 
-    for i in reversed(range(n)):
-        vg_wait(0, i)
+    bulk(fwd_slot(partner), near_recv.at[0]).wait_recv()
     weight_term(0)
     for i in reversed(range(n)):
         if chips > 1:
-            vg_wait(1, i)
+            bulk(vg_slot(chip_peer(1), i), vg_arrival(1, i)).wait_recv()
         for c in evens:
             if c + 1 < chips:
                 relay_copy(c + 1, 0, i).start()
         for c in evens:
-            vg_wait(c, i)
+            bulk(vg_slot(chip_peer(c), i), vg_arrival(c, i)).wait_recv()
             if c + 1 < chips:
                 relay_copy(c + 1, 1, i).start()
         if i == n // 2:
-            for off in early:
+            for off in outgoing[:EARLY]:
                 out_start(off)
-    for off in outgoing:
-        if off not in early:
-            out_start(off)
     for c in direct:
         if c:
             fwd_copy(c, chip_peer(c)).start()
+    for off in outgoing[EARLY:MIDDLE]:
+        out_start(off)
     for c in direct:
         if c:
-            fwd_copy(c, flip(chip, c, chips) * CORES + (1 - core)).wait_recv()
+            bulk(fwd_slot(flip(chip, c, chips) * CORES + (1 - core)), fwd_recv.at[c]).wait_recv()
             weight_term(c)
-    for c in range(chips):
-        if c not in direct:
-            for i in reversed(range(n)):
-                relay_wait(c, 0, i)
-                relay_wait(c, 1, i)
-            fwd_copy(c, chip_peer(c)).start()
-            fwd_copy(c, flip(chip, c, chips) * CORES + (1 - core)).wait_recv()
-            weight_term(c)
-
-    for c in direct + [c for c in range(chips) if c not in direct]:
+    relayed = [c for c in range(chips) if c not in direct]
+    for c in relayed:
+        bulk(fwd_slot(chip_peer(c)), relay_recv.at[c // 2]).wait_recv()
+        fwd_copy(c, chip_peer(c)).start()
+    for off in outgoing[MIDDLE:]:
+        out_start(off)
+    for c in relayed:
+        bulk(fwd_slot(flip(chip, c, chips) * CORES + (1 - core)), fwd_recv.at[c]).wait_recv()
+        weight_term(c)
+
+    for c in direct + relayed:
         value = zs[c, dme].astype(jnp.float32)
+        bulk(zr.at[c, pl.ds(0, ndp - 1)], z_recv.at[c]).wait_recv()
         for off in range(1, ndp):
-            z_wait(c, off)
             value = value + zr[c, lax.rem(dme + ndp - off, ndp)].astype(jnp.float32)
         dw_out[:, at(flip(chip, c, chips), width)] = value * total_tokens ** (-0.5)
 
-    for off in order:
-        dq_copy(off, True).wait()
-        dk_copy(off, True).wait()
+    for index, ref in enumerate((dqs, dks)):
+        bulk(ref.at[pl.ds(0, n - 1)], out_recv.at[index]).wait_recv()
     dq_local().wait()
     dk_local().wait()
 
@@ -377,20 +382,14 @@
             total = total + rdk[other].astype(jnp.float32)
         dk_out[...] = total.astype(jnp.bfloat16)
 
-    for off in order:
-        for kind in range(6):
-            input_copy(kind, off).wait_send()
-    for c in range(chips):
-        for i in range(n):
-            if c in direct:
-                vg_copy(c, i).wait_send()
-            else:
-                relay_copy(c, 0, i).wait_send()
-                relay_copy(c, 1, i).wait_send()
-        if c:
-            fwd_copy(c, chip_peer(c)).wait_send()
-        for off in range(1, ndp):
-            z_copy(c, off).wait_send()
+    for kind in range(6):
+        bulk(others[kind], in_send.at[kind]).wait_send()
+    for index, ref in enumerate((dqs, dks)):
+        bulk(ref.at[pl.ds(0, n - 1)], out_send.at[index]).wait_send()
+    for index, count in enumerate((len(direct), len(relayed), chips - 1)):
+        if count:
+            bulk(vg.at[0, :, pl.ds(0, count * hw)], vg_send.at[index]).wait_send()
+    bulk(zs.at[:, pl.ds(0, ndp - 1)], vg_send.at[3]).wait_send()
 
 
 def solution(mesh):
@@ -445,11 +444,10 @@
                 pltpu.VMEM((rows, width), f32),
                 pltpu.VMEM((chips, ndp, piece, width), bf),
                 pltpu.VMEM((chips, ndp, piece, width), bf),
-                dma((7,)), dma((6, n)), dma((6, n)), dma((8,)),
-                dma((n,)), dma((n,)), dma((n,)), dma((n,)),
-                dma((chips, n)), dma((chips, n)),
-                dma((chips, 2, n)), dma((chips, 2, n)), dma((chips,)), dma((chips,)),
-                dma((chips, ndp)), dma((chips, ndp)),
+                dma((7,)), dma((6,)), dma((6,)), dma((8,)), dma((2,)), dma((2,)),
+                dma((4,)), dma((1,)), dma((chips // 2, n)), dma((chips // 2,)), dma((chips,)), dma((chips,)),
+                pltpu.SemaphoreType.REGULAR((max(1, n.bit_length() - 2), n.bit_length() - 1)),
+                pltpu.SemaphoreType.REGULAR((max(1, ndp - 2), 2)),
             ],
             compiler_params=pltpu.CompilerParams(
                 collective_id=0, has_side_effects=True, vmem_limit_bytes=60 * 1024 * 1024

time: 55.4 us -> 53.6 us (0.968)
  Pallas kernels: 52.2 us -> 50.3 us
    pallas_call x1, Pallas kernels: 52.2 us -> 50.3 us  [local(): pl.pallas_call(functools.partial(kernel, n, ndp, float(ndp * seq)), out_s...]
where the time goes in v2:
time: 53.6 us; the launch traced here: 53.1 us
  Pallas kernels  50.3 us (94%)
  local copies, waits for them, and re-layouts  2.21 us (4%)
  between operations  0.64 us (1%)
    pallas_call x1, Pallas kernels, local(): pl.pallas_call(functools.partial(kernel, n, ndp, float(ndp * seq)), out_s...  50.3 us
    unnamed x3, local copies, waits for them, and re-layouts  2.21 us

profile of v2, /device:TPU:1, one launch (start us, length us, event | category | flops | bytes accessed | tf_op | source)
XLA Modules:
  0.0 53.1 jit_solution(13621881467915398220)
XLA Ops:
  0.6 50.3 %attention_backward.1 = (bf16[128,2048]{1,0:T(8,128)(2,1)S(1)}, bf16[128,1024]{1,0:T(8,128)(2,1)S(1)}, f32[72,1024]{1,0:T(8,128)S(1)}) custom-call(bf16[128,2304]{1,0:T(8,128)(2,1)} %bitcast.10, bf16[128,2048]{1,0:T(8,128)(2,1)} %bitcast.11, bf16[128,1024]{1,0:T(8,128)(2,1)} %bitcast.14, bf16[128,1024]{1,0:T(8,128)(2,1)} %bitcast.15, ...), custom_call_target="tpu_custom_call" | custom-call | tf_op jit(solution)/shard_map/attention_backward/pallas_call | solution.py:412
  50.9 0.8 %copy.13 = bf16[1,128,2048]{2,1,0:T(8,128)(2,1)} copy(bf16[1,128,2048]{2,1,0:T(8,128)(2,1)S(1)} %bitcast.8) | data formatting | bytes 1048576
  51.7 0.7 %copy.14 = bf16[1,128,1024]{2,1,0:T(8,128)(2,1)} copy(bf16[1,128,1024]{2,1,0:T(8,128)(2,1)S(1)} %bitcast.9) | data formatting | bytes 524288
  52.4 0.7 %copy.15 = f32[72,1024]{1,0:T(8,128)} copy(f32[72,1024]{1,0:T(8,128)S(1)} %get-tuple-element.11) | data formatting | bytes 589824

commit v3 on v2

--- a/solution.py
+++ b/solution.py
@@ -11,7 +11,7 @@
 KEY_VALUE_HEADS = 8
 HEAD_WIDTH = 128
 CORES = 2
-EARLY, MIDDLE = 2, 2
+EARLY, MIDDLE = 2, 4
 MESH = pl.DeviceIdType.MESH
 
 query_scale = 144.0 ** (-0.5)
@@ -48,7 +48,7 @@
     rq, rk, rv, rdo, meta, rmeta, xt, rx, dock,
     dk_acc, dv_acc, dqs, dks, rdk, vg, pf, zs, zr,
     load_sem, in_send, in_recv, local_sem, out_send, out_recv, vg_send, near_recv, vg_recv,
-    relay_recv, fwd_recv, z_recv, seq_sem, dp_sem,
+    relay_recv, fwd_recv, z_recv, dp_sem,
 ):
     me = lax.axis_index("seq")
     dme = lax.axis_index("dp")
@@ -66,11 +66,10 @@
     chip, core = me // CORES, lax.rem(me, CORES)
     partner = chip * CORES + (1 - core)
 
-    bits = [1 << b for b in range(n.bit_length() - 1)]
     below, above = dme > 0, dme < ndp - 1
     barrier = pltpu.get_barrier_semaphore()
-    for bit in reversed(bits):
-        pl.semaphore_signal(barrier, inc=1, device_id={"seq": flip(me, bit, n)}, device_id_type=MESH)
+    for off in range(n - 1, 0, -1):
+        pl.semaphore_signal(barrier, inc=1, device_id={"seq": flip(me, off, n)}, device_id_type=MESH)
 
     def tell_dp(up, down):
         @pl.when(above)
@@ -148,21 +147,13 @@
         xt[span, :] = x_ref[:, span].astype(jnp.float32).T.astype(jnp.bfloat16)
     for load in loads[4:]:
         load.wait()
-    pl.semaphore_wait(barrier, len(bits) + below.astype(jnp.int32) + above.astype(jnp.int32))
-
-    for distance in range(1, len(bits) + 1):
-        if distance > 1:
-            for b, bit in enumerate(bits):
-                pl.semaphore_signal(
-                    seq_sem.at[distance - 2, b], inc=1, device_id={"seq": flip(me, bit, n)}, device_id_type=MESH
-                )
-            for b in range(len(bits)):
-                pl.semaphore_wait(seq_sem.at[distance - 2, b], 1)
-        for off in range(n - 1, 0, -1):
-            if off.bit_count() == distance:
-                for kind in range(5):
-                    input_copy(kind, off).start()
-    for off in range(n - 1, 0, -1):
+    pl.semaphore_wait(barrier, n - 1 + below.astype(jnp.int32) + above.astype(jnp.int32))
+
+    order = list(range(n - 1, 0, -1))
+    for off in order:
+        for kind in range(5):
+            input_copy(kind, off).start()
+    for off in order:
         input_copy(5, off).start()
     own_copy(4).start()
     own_copy(5).start()
@@ -446,7 +437,6 @@
                 pltpu.VMEM((chips, ndp, piece, width), bf),
                 dma((7,)), dma((6,)), dma((6,)), dma((8,)), dma((2,)), dma((2,)),
                 dma((4,)), dma((1,)), dma((chips // 2, n)), dma((chips // 2,)), dma((chips,)), dma((chips,)),
-                pltpu.SemaphoreType.REGULAR((max(1, n.bit_length() - 2), n.bit_length() - 1)),
                 pltpu.SemaphoreType.REGULAR((max(1, ndp - 2), 2)),
             ],
             compiler_params=pltpu.CompilerParams(
@@ -454,6 +444,25 @@
             ),
             name="attention_backward",
         )(normed_input[0], queries[0], keys[0], values[0], saved_output[0], cotangent[0], doc_ids)
+        def finish(*refs):
+            copies_out = [
+                pltpu.make_async_copy(src, dst, refs[6].at[index])
+                for index, (src, dst) in enumerate(zip(refs[:3], refs[3:6]))
+            ]
+            for copy in copies_out:
+                copy.start()
+            for copy in copies_out:
+                copy.wait()
+
+        anywhere = pl.BlockSpec(memory_space=pl.ANY)
+        dq, dk, dw = pl.pallas_call(
+            finish,
+            out_shape=tuple(jax.ShapeDtypeStruct(part.shape, part.dtype) for part in (dq, dk, dw)),
+            in_specs=[anywhere] * 3,
+            out_specs=(anywhere,) * 3,
+            scratch_shapes=[dma((3,))],
+            name="finish",
+        )(pltpu.with_memory_space_constraint(dq, pltpu.VMEM), pltpu.with_memory_space_constraint(dk, pltpu.VMEM), pltpu.with_memory_space_constraint(dw, pltpu.VMEM))
         return dq[None], dk[None], dw
 
     spec = P("dp", "seq", None)

time: 53.6 us -> 51 us (0.951)
  local copies, waits for them, and re-layouts: 2.21 us -> 0 us
    unnamed x3 -> x0, local copies, waits for them, and re-layouts: 2.21 us -> none
    pallas_call x1, Pallas kernels: 50.3 us -> 49.2 us  [local(): pl.pallas_call(functools.partial(kernel, n, ndp, float(ndp * seq)), out_s...]
    pallas_call x0 -> x1, Pallas kernels: none -> 1 us  [local(): pl.pallas_call(finish, out_shape=tuple((jax.ShapeDtypeStruct(part.shape,...]
where the time goes in v3:
time: 51 us; the launch traced here: 50.8 us
  Pallas kernels  50.2 us (98%)
  between operations  0.64 us (1%)
    pallas_call x1, Pallas kernels, local(): pl.pallas_call(functools.partial(kernel, n, ndp, float(ndp * seq)), out_s...  49.2 us

profile of v3, /device:TPU:1, one launch (start us, length us, event | category | flops | bytes accessed | tf_op | source)
XLA Modules:
  0.0 50.8 jit_solution(13624971063258439468)
XLA Ops:
  0.6 49.2 %attention_backward.1 = (bf16[128,2048]{1,0:T(8,128)(2,1)S(1)}, bf16[128,1024]{1,0:T(8,128)(2,1)S(1)}, f32[72,1024]{1,0:T(8,128)S(1)}) custom-call(bf16[128,2304]{1,0:T(8,128)(2,1)} %bitcast.8, bf16[128,2048]{1,0:T(8,128)(2,1)} %bitcast.9, bf16[128,1024]{1,0:T(8,128)(2,1)} %bitcast.12, bf16[128,1024]{1,0:T(8,128)(2,1)} %bitcast.13, ...), custom_call_target="tpu_custom_call" | custom-call | tf_op jit(solution)/shard_map/attention_backward/pallas_call | solution.py:403
  49.8 1.0 %finish.1 = (bf16[128,2048]{1,0:T(8,128)(2,1)}, bf16[128,1024]{1,0:T(8,128)(2,1)}, f32[72,1024]{1,0:T(8,128)}) custom-call(bf16[128,2048]{1,0:T(8,128)(2,1)S(1)} %get-tuple-element.9.refs_0_, bf16[128,1024]{1,0:T(8,128)(2,1)S(1)} %get-tuple-element.10.refs_1_, f32[72,1024]{1,0:T(8,128)S(1)} %get-tuple-element.11.refs_2_), custom_call_target="tpu_custom_call" | custom-call | tf_op jit(solution)/shard_map/finish/pallas_call | solution.py:458

commit v4 on v3

--- a/solution.py
+++ b/solution.py
@@ -12,6 +12,7 @@
 HEAD_WIDTH = 128
 CORES = 2
 EARLY, MIDDLE = 2, 4
+FIRST = 4
 MESH = pl.DeviceIdType.MESH
 
 query_scale = 144.0 ** (-0.5)
@@ -46,7 +47,7 @@
     dq_out, dk_out, dw_out,
     x_ref, q_ref, k_ref, v_ref, o_ref, do_ref, doc_ref,
     rq, rk, rv, rdo, meta, rmeta, xt, rx, dock,
-    dk_acc, dv_acc, dqs, dks, rdk, vg, pf, zs, zr,
+    dk_acc, dv_acc, kept_t, kept_w, kept_i, dqs, dks, rdk, vg, pf, zs, zr,
     load_sem, in_send, in_recv, local_sem, out_send, out_recv, vg_send, near_recv, vg_recv,
     relay_recv, fwd_recv, z_recv, dp_sem,
 ):
@@ -247,15 +248,18 @@
     causal = lax.broadcasted_iota(jnp.int32, (tokens, tokens), 0) <= lax.broadcasted_iota(
         jnp.int32, (tokens, tokens), 1
     )
+    def stacked(ref, i):
+        return jnp.concatenate([ref[at(i, tokens), g * hw : (g + 1) * hw] for g in range(hq)], axis=0)
+
+    windows = [range(max(0, i - reach), i + 1) for i in range(n)]
+    pairs = {pair: slot for slot, pair in enumerate((i, j) for i in range(n) for j in windows[i])}
+
     for i in reversed(range(n)):
         here = at(i, tokens)
-        q2 = jnp.concatenate([rq[here, g * hw : (g + 1) * hw] for g in range(hq)], axis=0)
-        do2 = jnp.concatenate([rdo[here, g * hw : (g + 1) * hw] for g in range(hq)], axis=0)
-        delta = jnp.concatenate([rmeta[i, g : g + 1, :] for g in range(hq)], axis=1)
+        q2, do2 = stacked(rq, i), stacked(rdo, i)
         docq = rmeta[i, hq : hq + 1, :]
-        window = range(max(0, i - reach), i + 1)
-        kept, totals = {}, jnp.zeros((1, hq * tokens), jnp.float32)
-        for j in window:
+        totals = jnp.zeros((1, hq * tokens), jnp.float32)
+        for j in windows[i]:
             t = jnp.tanh(nt(rk[at(j, tokens), :], q2) * (query_scale / soft_cap))
             allowed = dock[at(j, tokens), :] == docq
             if i == j:
@@ -263,41 +267,45 @@
             mask = jnp.where(allowed, 1.0, 0.0)
             w = jnp.exp(soft_cap * t) * jnp.concatenate([mask] * hq, axis=1)
             totals = totals + jnp.sum(w, axis=0, keepdims=True)
-            kept[j] = (t, w)
+            kept_t[pairs[i, j]] = t
+            kept_w[pairs[i, j]] = w
         inverse = 1.0 / totals
-        dq = jnp.zeros((hq * tokens, hw), jnp.float32)
-        for j in window:
-            t, w = kept[j]
-            kj = rk[at(j, tokens), :]
-            p = w * inverse
-            ds = p * (nt(rv[at(j, tokens), :], do2) - delta) * ((1.0 - t * t) * query_scale)
-            ds16, p16 = ds.astype(jnp.bfloat16), p.astype(jnp.bfloat16)
-            dk_term = jnp.dot(ds16, q2, preferred_element_type=jnp.float32)
+        kept_i[i] = inverse
+        for j in windows[i]:
+            p16 = (kept_w[pairs[i, j]] * inverse).astype(jnp.bfloat16)
             dv_term = jnp.dot(p16, do2, preferred_element_type=jnp.float32)
             if i == min(n - 1, j + reach):
-                dk_acc[at(j, tokens), :] = dk_term
                 dv_acc[at(j, tokens), :] = dv_term
             else:
+                dv_acc[at(j, tokens), :] += dv_term
+        vg[lax.rem(me, copies), at(i, tokens), at(me // copies, hw)] = dv_acc[here, :].astype(jnp.bfloat16)
+        for c in reversed(direct):
+            vg_copy(c, i).start()
+
+    def scores_back(i):
+        q2, do2 = stacked(rq, i), stacked(rdo, i)
+        delta = jnp.concatenate([rmeta[i, g : g + 1, :] for g in range(hq)], axis=1)
+        dq = jnp.zeros((hq * tokens, hw), jnp.float32)
+        for j in windows[i]:
+            t = kept_t[pairs[i, j]]
+            p = kept_w[pairs[i, j]] * kept_i[i]
+            ds = p * (nt(rv[at(j, tokens), :], do2) - delta) * ((1.0 - t * t) * query_scale)
+            ds16 = ds.astype(jnp.bfloat16)
+            dk_term = jnp.dot(ds16, q2, preferred_element_type=jnp.float32)
+            if i == min(n - 1, j + reach):
+                dk_acc[at(j, tokens), :] = dk_term
+            else:
                 dk_acc[at(j, tokens), :] += dk_term
-                dv_acc[at(j, tokens), :] += dv_term
-            dq = dq + tn(ds16, kj)
-        vg[lax.rem(me, copies), at(i, tokens), at(me // copies, hw)] = dv_acc[here, :].astype(jnp.bfloat16)
+            dq = dq + tn(ds16, rk[at(j, tokens), :])
         for g in range(hq):
             dqs[i, :, g * hw : (g + 1) * hw] = dq[g * tokens : (g + 1) * tokens].astype(jnp.bfloat16)
-        dks[i] = dk_acc[here, :].astype(jnp.bfloat16)
-        for c in reversed(direct):
-            vg_copy(c, i).start()
+        dks[i] = dk_acc[at(i, tokens), :].astype(jnp.bfloat16)
 
     def out_start(off):
         dq_copy(off).start()
         dk_copy(off).start()
 
     outgoing = list(range(3, n, 2)) + list(range(2, n, 2)) + [1]
-    dq_local().start()
-    dk_local().start()
-
-    own_copy(5).wait()
-    bulk(others[5], in_recv.at[5]).wait_recv()
 
     def z_copy(c, off):
         dest = lax.rem(dme + off, ndp)
@@ -321,8 +329,15 @@
         for off in range(1, ndp):
             z_copy(c, off).start()
 
-    bulk(fwd_slot(partner), near_recv.at[0]).wait_recv()
-    weight_term(0)
+    for i in reversed(range(n)):
+        scores_back(i)
+        if i == FIRST:
+            own_copy(5).wait()
+            bulk(others[5], in_recv.at[5]).wait_recv()
+            bulk(fwd_slot(partner), near_recv.at[0]).wait_recv()
+            weight_term(0)
+    dq_local().start()
+    dk_local().start()
     for i in reversed(range(n)):
         if chips > 1:
             bulk(vg_slot(chip_peer(1), i), vg_arrival(1, i)).wait_recv()
@@ -397,6 +412,8 @@
         piece = rows // ndp
         chips = n // CORES
         width = CORES * hw // copies
+        reach = (seq // 2 - 1 + tokens - 1) // tokens
+        pairs = sum(min(i, reach) + 1 for i in range(n))
         bf, f32 = jnp.bfloat16, jnp.float32
         dma = pltpu.SemaphoreType.DMA
         vmem = pl.BlockSpec(memory_space=pltpu.VMEM)
@@ -428,6 +445,9 @@
                 pltpu.VMEM((seq, tokens), f32),
                 pltpu.VMEM((seq, hw), f32),
                 pltpu.VMEM((seq, hw), f32),
+                pltpu.VMEM((pairs, tokens, hq * tokens), f32),
+                pltpu.VMEM((pairs, tokens, hq * tokens), f32),
+                pltpu.VMEM((n, 1, hq * tokens), f32),
                 pltpu.VMEM((n, tokens, hq * hw), bf),
                 pltpu.VMEM((n, tokens, hw), bf),
                 pltpu.VMEM((copies, tokens, kvw), bf),

time: 51 us -> 50.5 us (level)
  no operation moved by 1% of the time
where the time goes in v4:
time: 50.5 us; the launch traced here: 50.3 us
  Pallas kernels  49.7 us (98%)
  between operations  0.64 us (1%)
    pallas_call x1, Pallas kernels, local(): pl.pallas_call(functools.partial(kernel, n, ndp, float(ndp * seq)), out_s...  48.7 us

profile of v4, /device:TPU:1, one launch (start us, length us, event | category | flops | bytes accessed | tf_op | source)
XLA Modules:
  0.0 50.3 jit_solution(6336632363583860103)
XLA Ops:
  0.6 48.7 %attention_backward.1 = (bf16[128,2048]{1,0:T(8,128)(2,1)S(1)}, bf16[128,1024]{1,0:T(8,128)(2,1)S(1)}, f32[72,1024]{1,0:T(8,128)S(1)}) custom-call(bf16[128,2304]{1,0:T(8,128)(2,1)} %bitcast.8, bf16[128,2048]{1,0:T(8,128)(2,1)} %bitcast.9, bf16[128,1024]{1,0:T(8,128)(2,1)} %bitcast.12, bf16[128,1024]{1,0:T(8,128)(2,1)} %bitcast.13, ...), custom_call_target="tpu_custom_call" | custom-call | tf_op jit(solution)/shard_map/attention_backward/pallas_call | solution.py:420
  49.3 1.0 %finish.1 = (bf16[128,2048]{1,0:T(8,128)(2,1)}, bf16[128,1024]{1,0:T(8,128)(2,1)}, f32[72,1024]{1,0:T(8,128)}) custom-call(bf16[128,2048]{1,0:T(8,128)(2,1)S(1)} %get-tuple-element.9.refs_0_, bf16[128,1024]{1,0:T(8,128)(2,1)S(1)} %get-tuple-element.10.refs_1_, f32[72,1024]{1,0:T(8,128)S(1)} %get-tuple-element.11.refs_2_), custom_call_target="tpu_custom_call" | custom-call | tf_op jit(solution)/shard_map/finish/pallas_call | solution.py:478

commit v5 on v4

--- a/solution.py
+++ b/solution.py
@@ -17,6 +17,7 @@
 
 query_scale = 144.0 ** (-0.5)
 soft_cap = 50.0
+LOG2E = 1.4426950408889634
 
 
 def flip(index, mask, count):
@@ -265,7 +266,7 @@
             if i == j:
                 allowed = allowed & causal
             mask = jnp.where(allowed, 1.0, 0.0)
-            w = jnp.exp(soft_cap * t) * jnp.concatenate([mask] * hq, axis=1)
+            w = jnp.exp2((soft_cap * LOG2E) * t) * jnp.concatenate([mask] * hq, axis=1)
             totals = totals + jnp.sum(w, axis=0, keepdims=True)
             kept_t[pairs[i, j]] = t
             kept_w[pairs[i, j]] = w
@@ -289,7 +290,7 @@
         for j in windows[i]:
             t = kept_t[pairs[i, j]]
             p = kept_w[pairs[i, j]] * kept_i[i]
-            ds = p * (nt(rv[at(j, tokens), :], do2) - delta) * ((1.0 - t * t) * query_scale)
+            ds = p * (nt(rv[at(j, tokens), :], do2) - delta) * (1.0 - t * t)
             ds16 = ds.astype(jnp.bfloat16)
             dk_term = jnp.dot(ds16, q2, preferred_element_type=jnp.float32)
             if i == min(n - 1, j + reach):
@@ -298,8 +299,8 @@
                 dk_acc[at(j, tokens), :] += dk_term
             dq = dq + tn(ds16, rk[at(j, tokens), :])
         for g in range(hq):
-            dqs[i, :, g * hw : (g + 1) * hw] = dq[g * tokens : (g + 1) * tokens].astype(jnp.bfloat16)
-        dks[i] = dk_acc[at(i, tokens), :].astype(jnp.bfloat16)
+            dqs[i, :, g * hw : (g + 1) * hw] = (dq[g * tokens : (g + 1) * tokens] * query_scale).astype(jnp.bfloat16)
+        dks[i] = (dk_acc[at(i, tokens), :] * query_scale).astype(jnp.bfloat16)
 
     def out_start(off):
         dq_copy(off).start()

time: 50.5 us -> 50.5 us (level)
  no operation moved by 1% of the time
where the time goes in v5:
time: 50.5 us; the launch traced here: 50.3 us
  Pallas kernels  49.7 us (98%)
  between operations  0.64 us (1%)
    pallas_call x1, Pallas kernels, local(): pl.pallas_call(functools.partial(kernel, n, ndp, float(ndp * seq)), out_s...  48.7 us

profile of v5, /device:TPU:1, one launch (start us, length us, event | category | flops | bytes accessed | tf_op | source)
XLA Modules:
  0.0 50.3 jit_solution(10319628040908696407)
XLA Ops:
  0.6 48.7 %attention_backward.1 = (bf16[128,2048]{1,0:T(8,128)(2,1)S(1)}, bf16[128,1024]{1,0:T(8,128)(2,1)S(1)}, f32[72,1024]{1,0:T(8,128)S(1)}) custom-call(bf16[128,2304]{1,0:T(8,128)(2,1)} %bitcast.8, bf16[128,2048]{1,0:T(8,128)(2,1)} %bitcast.9, bf16[128,1024]{1,0:T(8,128)(2,1)} %bitcast.12, bf16[128,1024]{1,0:T(8,128)(2,1)} %bitcast.13, ...), custom_call_target="tpu_custom_call" | custom-call | tf_op jit(solution)/shard_map/attention_backward/pallas_call | solution.py:421
  49.3 1.0 %finish.1 = (bf16[128,2048]{1,0:T(8,128)(2,1)}, bf16[128,1024]{1,0:T(8,128)(2,1)}, f32[72,1024]{1,0:T(8,128)}) custom-call(bf16[128,2048]{1,0:T(8,128)(2,1)S(1)} %get-tuple-element.9.refs_0_, bf16[128,1024]{1,0:T(8,128)(2,1)S(1)} %get-tuple-element.10.refs_1_, f32[72,1024]{1,0:T(8,128)S(1)} %get-tuple-element.11.refs_2_), custom_call_target="tpu_custom_call" | custom-call | tf_op jit(solution)/shard_map/finish/pallas_call | solution.py:479
